TPU v7x, 32 devices: a whole 2x2x4 slice. The times are simulated.
32 devices in a mesh: row: 2 (over y), col: 4 (over x, core), band: 4 (over z).
Axes of the slice: x: 2, y: 2, z: 4, core: 2. Of those that a mesh axis runs over, the one named last changes fastest.
Arguments:
- noisy: float32 [224, 32, 4096], P('band', 'row', 'col'), may hold values from -4 to 4
- weight_map: float32 [32, 4096], P('row', 'col'), may hold values from 1.5 to 12
Outputs:
- denoised: float32 [224, 32, 4096], P('band', 'row', 'col')
All inputs are finite; a program needn't handle non-finite values.
Results may differ from a plain program's by a relative error of at most 0.0001.
Values sent between devices are 32-bit elements; how exact they have to be, the bound alone decides.
A program may use at most 64 MiB of HBM per device.

v0:
```python
import functools

import jax
import jax.numpy as jnp
from jax import lax
from jax.experimental import pallas as pl
from jax.experimental.pallas import tpu as pltpu
from jax.sharding import PartitionSpec as P

ITERS = 4
dual_step = 0.35
primal_step = 0.35
KEEP = 1.0 / (1.0 + primal_step)
GAIN = primal_step / (1.0 + primal_step)
STEP = GAIN * dual_step
LANES = 128
MESH = pl.DeviceIdType.MESH


def kernel(n_row, n_col, n_band, x_ref, w_ref, out_ref,
           N, U, W, QX, QY, HU, HD, E, ER, EL, WT, SC, CY, S, SE, R, RE,
           LA, LB, FA, FB, MA, MB,
           in_sem, out_sem, ys, yr, xs, xr, zs, zr):
    bands, rows, cols = x_ref.shape
    wide = cols + LANES
    groups = bands // 8
    last = rows - 1
    ri = lax.axis_index("row")
    ci = lax.axis_index("col")
    bi = lax.axis_index("band")
    has_up = ri > 0
    has_down = ri < n_row - 1
    has_left = ci > 0
    has_right = ci < n_col - 1

    fetches = [pltpu.make_async_copy(x_ref.at[:, r, :], N.at[r, 0:bands, 0:cols], in_sem.at[r])
               for r in range(rows)]
    for copy in fetches:
        copy.start()

    barrier = pltpu.get_barrier_semaphore()
    for cond, axis, target in ((has_up, "row", ri - 1), (has_down, "row", ri + 1),
                               (has_left, "col", ci - 1), (has_right, "col", ci + 1)):
        @pl.when(cond)
        def _():
            pl.semaphore_signal(barrier, inc=1, device_id={axis: target}, device_id_type=MESH)
    for d in range(1, n_band):
        pl.semaphore_signal(barrier, inc=1, device_id={"band": lax.rem(bi + d, n_band)}, device_id_type=MESH)
    count = (n_band - 1 + has_up.astype(jnp.int32) + has_down.astype(jnp.int32)
             + has_left.astype(jnp.int32) + has_right.astype(jnp.int32))

    def up_copy(i, src, dst):
        return pltpu.make_async_remote_copy(
            src_ref=src, dst_ref=dst, send_sem=ys.at[0, i], recv_sem=yr.at[0, i],
            device_id={"row": ri - 1}, device_id_type=MESH)

    def down_copy(i, src, dst):
        return pltpu.make_async_remote_copy(
            src_ref=src, dst_ref=dst, send_sem=ys.at[1, i], recv_sem=yr.at[1, i],
            device_id={"row": ri + 1}, device_id_type=MESH)

    def y_pair(k, part):
        if k == 0:
            span = pl.ds(0, cols) if part == 0 else pl.ds(cols, LANES)
            i = 0 if part == 0 else ITERS
            return (up_copy(i, N.at[0, :, span], HU.at[0, :, span]),
                    down_copy(i, N.at[last, :, span], HD.at[0, :, span]))
        span = pl.ds(0, bands)
        return (up_copy(k, W.at[0], HU.at[k, span]), down_copy(k, W.at[last], HD.at[k, span]))

    def y_start(k, part=0):
        up, down = y_pair(k, part)

        @pl.when(has_up)
        def _():
            up.start()

        @pl.when(has_down)
        def _():
            down.start()

    def y_recv(k, part=0):
        up, down = y_pair(k, part)

        @pl.when(has_down)
        def _():
            up.wait_recv()

        @pl.when(has_up)
        def _():
            down.wait_recv()

    def y_sent(k, part=0):
        up, down = y_pair(k, part)

        @pl.when(has_up)
        def _():
            up.wait_send()

        @pl.when(has_down)
        def _():
            down.wait_send()

    def z_copy(k, d, part):
        if part < 2:
            half = pl.ds(part * 8, 8)
            src, dst = S.at[k, half], R.at[k, d - 1, half]
        else:
            src, dst = SE.at[k], RE.at[k, d - 1]
        return pltpu.make_async_remote_copy(
            src_ref=src, dst_ref=dst, send_sem=zs.at[k, d - 1, part], recv_sem=zr.at[k, d - 1, part],
            device_id={"band": lax.rem(bi + d, n_band)}, device_id_type=MESH)

    def z_start(k, part):
        for d in range(1, n_band):
            z_copy(k, d, part).start()

    def total(k, part):
        for d in range(1, n_band):
            z_copy(k, d, part).wait_recv()
        if part < 2:
            half = pl.ds(part * 8, 8)
            acc = S[k, half]
            for d in range(1, n_band):
                acc = acc + R[k, d - 1, half]
            return acc
        acc = SE[k]
        for d in range(1, n_band):
            acc = acc + RE[k, d - 1]
        return acc

    def scale_of(weight, squares):
        return weight / jnp.maximum(weight, jnp.sqrt(1.0 + squares * (1.0 / (GAIN * GAIN))))

    def put_scale(r, v):
        SC[r] = jnp.broadcast_to(v, (8, wide))

    def sync(k):
        for part in range(2):
            half = pl.ds(part * 8, 8)
            values = scale_of(WT[half], total(k, part))
            for i in range(8):
                if part * 8 + i < last:
                    put_scale(part * 8 + i, values[i:i + 1])
        edge = total(k, 2)
        put_scale(last, scale_of(WT[pl.ds(last, 1)], edge[0:1]))
        put_scale(rows, scale_of(WT[pl.ds(rows, 1)], edge[1:2]))

    tiles = wide // LANES
    pitch_m = LA.shape[0] // tiles

    def tile(j):
        return pl.ds((j % tiles) * LANES, LANES)

    def part_of(F, j):
        at = (j % tiles) * pitch_m
        return F.at[pl.ds(at, bands), 0:LANES], F.at[pl.ds(at, bands), LANES:2 * LANES]

    def difference(L, F, M, load, neighbour):
        for j in range(tiles):
            v = load(j)
            high = v.astype(jnp.bfloat16)
            low = (v - high.astype(jnp.float32)).astype(jnp.bfloat16)
            L[pl.ds(j * pitch_m, bands), 0:LANES] = high
            L[pl.ds(j * pitch_m, bands), LANES:2 * LANES] = low
        F[...] = jnp.dot(L[...], M[...], preferred_element_type=jnp.float32)
        return lambda j: part_of(F, j)[0][...] + part_of(F, j + neighbour)[1][...]

    def right_diff(load):
        return difference(LA, FA, MA, load, 1)

    def left_diff(load):
        return difference(LB, FB, MB, load, -1)

    at_in = lax.broadcasted_iota(jnp.int32, (2 * LANES, 2 * LANES), 0) % LANES
    at_out = lax.broadcasted_iota(jnp.int32, (2 * LANES, 2 * LANES), 1)

    def plus(cond):
        return jnp.where(cond, 1.0, 0.0)
    inside = at_out < LANES
    MA[...] = (plus(inside & (at_in == at_out + 1)) - plus(inside & (at_in == at_out))
               + plus((at_out == 2 * LANES - 1) & (at_in == 0))).astype(jnp.bfloat16)
    MB[...] = (plus(inside & (at_in == at_out)) - plus(inside & (at_in == at_out - 1))
               - plus((at_out == LANES) & (at_in == LANES - 1))).astype(jnp.bfloat16)
    LA[...] = jnp.zeros_like(LA)
    LB[...] = jnp.zeros_like(LB)

    pl.semaphore_wait(barrier, count)

    lane = lax.broadcasted_iota(jnp.int32, (1, wide), 1)
    column = ci * cols + jnp.where(lane < cols + LANES // 2, lane, lane - wide)
    CY[...] = jnp.where((column >= 0) & (column < n_col * cols - 1), STEP, 0.0)

    def put_weight(r, _):
        N[r, pl.ds(bands, 8), 0:cols] = jnp.broadcast_to(w_ref[pl.ds(r, 1), :], (8, cols))
        return 0
    lax.fori_loop(0, rows, put_weight, 0)
    S[:, pl.ds(8, 8), :] = jnp.zeros((ITERS, 8, wide), jnp.float32)

    @pl.when(jnp.logical_not(has_down))
    def _():
        HU[...] = jnp.zeros_like(HU)

    @pl.when(jnp.logical_not(has_up))
    def _():
        HD[...] = jnp.zeros_like(HD)

    @pl.when(jnp.logical_not(has_right))
    def _():
        ER[...] = jnp.zeros_like(ER)

    @pl.when(jnp.logical_not(has_left))
    def _():
        EL[...] = jnp.zeros_like(EL)

    for copy in fetches:
        copy.wait()
    y_start(0, 0)

    pitch = 2 * ITERS
    spot = lax.broadcasted_iota(jnp.int32, (8, LANES), 1)

    def pack(g, _):
        span = pl.ds(pl.multiple_of(g * 8, 8), 8)
        acc = jnp.zeros((8, LANES), jnp.float32)
        for r in range(rows):
            at = r * pitch
            head = pltpu.roll(N[r, span, 0:LANES], at % LANES, 1)
            tail = pltpu.roll(N[r, span, cols - LANES:cols], (at + pitch) % LANES, 1)
            acc = jnp.where((spot >= at) & (spot < at + ITERS), head, acc)
            acc = jnp.where((spot >= at + ITERS) & (spot < at + pitch), tail, acc)
        E[span] = acc
        return 0
    lax.fori_loop(0, groups + 1, pack, 0)

    to_left = pltpu.make_async_remote_copy(
        src_ref=E, dst_ref=ER, send_sem=xs.at[0], recv_sem=xr.at[0],
        device_id={"col": ci - 1}, device_id_type=MESH)
    to_right = pltpu.make_async_remote_copy(
        src_ref=E, dst_ref=EL, send_sem=xs.at[1], recv_sem=xr.at[1],
        device_id={"col": ci + 1}, device_id_type=MESH)

    @pl.when(has_left)
    def _():
        to_left.start()

    @pl.when(has_right)
    def _():
        to_right.start()

    @pl.when(has_right)
    def _():
        to_left.wait_recv()

    @pl.when(has_left)
    def _():
        to_right.wait_recv()

    def unpack(g, _):
        span = pl.ds(pl.multiple_of(g * 8, 8), 8)
        from_right, from_left = ER[span], EL[span]
        for r in range(rows):
            at = r * pitch
            head = pltpu.roll(from_right, (LANES - at) % LANES, 1)
            tail = pltpu.roll(from_left, (LANES - at - pitch) % LANES, 1)
            N[r, span, cols:wide] = jnp.where(spot < LANES // 2, head, tail)
        return 0
    lax.fori_loop(0, groups + 1, unpack, 0)
    y_start(0, 1)

    def put_wt(r, _):
        WT[pl.ds(r, 1)] = N[r, pl.ds(bands, 1), :]
        return 0
    lax.fori_loop(0, rows, put_wt, 0)

    full = pl.ds(0, bands)

    def dual_row(r, own, nxt, cx, first, put):
        grad = right_diff(own)
        sums = []
        for j in range(tiles):
            t = tile(j)
            qx = cx * (nxt(j) - own(j))
            qy = CY[:, t] * grad(j)
            if not first:
                sc = SC[r, 0:1, t]
                qx = sc * QX[r, :, t] + qx
                qy = sc * QY[r, :, t] + qy
            QX[r, :, t] = qx
            QY[r, :, t] = qy
            sums.append(jnp.sum(qx * qx + qy * qy, axis=0, keepdims=True))
        put(jnp.concatenate(sums, axis=1))

    def put_main(k, r):
        def put(v):
            S[k, pl.ds(r, 1)] = v
        return put

    def put_edge(k, i):
        def put(v):
            SE[k, pl.ds(i, 1)] = v
        return put

    cx_last = jnp.where(has_down, STEP, 0.0)
    cx_above = jnp.where(has_up, STEP, 0.0)

    def edges(k, field):
        y_recv(k, 0)
        if k == 0:
            y_recv(0, 1)
            WT[pl.ds(rows, 1)] = HD[0, pl.ds(bands, 1), :]
        dual_row(last, lambda j: field[last, full, tile(j)], lambda j: HU[k, full, tile(j)],
                 cx_last, k == 0, put_edge(k, 0))
        dual_row(rows, lambda j: HD[k, full, tile(j)], lambda j: field[0, full, tile(j)],
                 cx_above, k == 0, put_edge(k, 1))
        z_start(k, 2)

    def scaled_y(r):
        return left_diff(lambda j: SC[r, 0:1, tile(j)] * QY[r, :, tile(j)])

    def primal_tile(r, above, j, first, div_y):
        t = tile(j)
        pu = SC[above, 0:1, t] * QX[above, :, t]
        px = SC[r, 0:1, t] * QX[r, :, t]
        div = (px - pu) + div_y(j)
        given = N[r, full, t]
        if first:
            u = given
            new = given + div
        else:
            u = U[r, :, t]
            new = KEEP * u + (GAIN * given + div)
        U[r, :, t] = new
        return pu, new, u

    def primal_row(r, above, first):
        div_y = scaled_y(r)
        for j in range(tiles):
            _, new, u = primal_tile(r, above, j, first, div_y)
            W[r, :, tile(j)] = 2.0 * new - u

    def pairs(lo, hi, row):
        def two(i, _):
            row(lo + 2 * i, 0)
            row(lo + 2 * i + 1, 0)
            return 0
        lax.fori_loop(0, (hi - lo) // 2, two, 0)
        if (hi - lo) % 2:
            row(hi - 1, 0)

    def start_row(r, _):
        dual_row(r, lambda j: N[r, full, tile(j)], lambda j: N[r + 1, full, tile(j)], STEP, True, put_main(0, r))
        return 0
    lax.fori_loop(0, 8, start_row, 0)
    z_start(0, 0)
    lax.fori_loop(8, last, start_row, 0)
    z_start(0, 1)
    edges(0, N)
    sync(0)

    for k in range(1, ITERS):
        first = k == 1
        if k > 1:
            y_sent(k - 1)
        primal_row(0, rows, first)
        primal_row(last, last - 1, first)
        y_start(k)

        def both(r, _, first=first, k=k):
            div_y = scaled_y(r)
            grad = right_diff(lambda j: W[r - 1, :, tile(j)])
            sums = []
            for j in range(tiles):
                t = tile(j)
                pu, new, u = primal_tile(r, r - 1, j, first, div_y)
                w = 2.0 * new - u
                W[r, :, t] = w
                qx = pu + STEP * (w - W[r - 1, :, t])
                qy = SC[r - 1, 0:1, t] * QY[r - 1, :, t] + CY[:, t] * grad(j)
                QX[r - 1, :, t] = qx
                QY[r - 1, :, t] = qy
                sums.append(jnp.sum(qx * qx + qy * qy, axis=0, keepdims=True))
            S[k, pl.ds(r - 1, 1)] = jnp.concatenate(sums, axis=1)
            return 0
        pairs(1, 9, both)
        z_start(k, 0)
        pairs(9, last, both)
        dual_row(last - 1, lambda j: W[last - 1, :, tile(j)], lambda j: W[last, :, tile(j)],
                 STEP, False, put_main(k, last - 1))
        z_start(k, 1)
        edges(k, W)
        sync(k)

    def finish(r, above):
        div_y = scaled_y(r)
        for j in range(tiles):
            primal_tile(r, above, j, False, div_y)
        pltpu.make_async_copy(U.at[r, :, 0:cols], out_ref.at[r], out_sem.at[r]).start()

    finish(0, rows)

    def finish_row(r, _):
        finish(r, r - 1)
        return 0
    lax.fori_loop(1, rows, finish_row, 0)

    y_sent(0, 0)
    y_sent(0, 1)
    y_sent(ITERS - 1)

    @pl.when(has_left)
    def _():
        to_left.wait_send()

    @pl.when(has_right)
    def _():
        to_right.wait_send()
    for k in range(ITERS):
        for d in range(1, n_band):
            for part in range(3):
                z_copy(k, d, part).wait_send()

    def drain(r, _):
        pltpu.make_async_copy(U.at[r, :, 0:cols], out_ref.at[r], out_sem.at[r]).wait()
        return 0
    lax.fori_loop(0, rows, drain, 0)


def local(n_row, n_col, n_band, noisy, weight_map):
    bands, rows, cols = noisy.shape
    padded = -(-bands // 8) * 8
    x = noisy
    if padded != bands:
        x = jnp.pad(x, ((0, padded - bands), (0, 0), (0, 0)))
    wide = cols + LANES
    f32, bf16 = jnp.float32, jnp.bfloat16
    depth = wide // LANES * (-(-padded // 16) * 16)
    peers = n_band - 1
    dma = pltpu.SemaphoreType.DMA
    out = pl.pallas_call(
        functools.partial(kernel, n_row, n_col, n_band),
        out_shape=jax.ShapeDtypeStruct((rows, padded, cols), f32),
        in_specs=[pl.BlockSpec(memory_space=pl.ANY), pl.BlockSpec(memory_space=pltpu.VMEM)],
        out_specs=pl.BlockSpec(memory_space=pl.ANY),
        scratch_shapes=[
            pltpu.VMEM((rows, padded + 8, wide), f32),
            pltpu.VMEM((rows, padded, wide), f32),
            pltpu.VMEM((rows, padded, wide), f32),
            pltpu.VMEM((rows + 1, padded, wide), f32),
            pltpu.VMEM((rows + 1, padded, wide), f32),
            pltpu.VMEM((ITERS, padded + 8, wide), f32),
            pltpu.VMEM((ITERS, padded + 8, wide), f32),
            pltpu.VMEM((padded + 8, LANES), f32),
            pltpu.VMEM((padded + 8, LANES), f32),
            pltpu.VMEM((padded + 8, LANES), f32),
            pltpu.VMEM((rows + 8, wide), f32),
            pltpu.VMEM((rows + 1, 8, wide), f32),
            pltpu.VMEM((1, wide), f32),
            pltpu.VMEM((ITERS, rows, wide), f32),
            pltpu.VMEM((ITERS, 2, wide), f32),
            pltpu.VMEM((ITERS, peers, rows, wide), f32),
            pltpu.VMEM((ITERS, peers, 2, wide), f32),
            pltpu.VMEM((depth, 2 * LANES), bf16),
            pltpu.VMEM((depth, 2 * LANES), bf16),
            pltpu.VMEM((depth, 2 * LANES), f32),
            pltpu.VMEM((depth, 2 * LANES), f32),
            pltpu.VMEM((2 * LANES, 2 * LANES), bf16),
            pltpu.VMEM((2 * LANES, 2 * LANES), bf16),
            dma((rows,)), dma((rows,)),
            dma((2, ITERS + 1)), dma((2, ITERS + 1)),
            dma((2,)), dma((2,)),
            dma((ITERS, peers, 3)), dma((ITERS, peers, 3)),
        ],
        compiler_params=pltpu.CompilerParams(
            collective_id=0, has_side_effects=True, vmem_limit_bytes=48 * 1024 * 1024),
    )(x, weight_map)
    return jnp.transpose(out[:, :bands], (1, 0, 2))


def solution(mesh):
    placed = (P("band", "row", "col"), P("row", "col"))
    sizes = dict(mesh.shape)
    body = functools.partial(local, sizes["row"], sizes["col"], sizes["band"])
    return jax.shard_map(
        body, mesh=mesh, in_specs=placed, out_specs=P("band", "row", "col"), check_vma=False
    )
```

profile of v0, /device:TPU:0, one launch (start us, length us, event | category | flops | bytes accessed | tf_op | source)
XLA Modules:
  0.0 68.4 jit_solution(9912347191127237938)
XLA Ops:
  0.0 0.0 copy-start
  0.0 0.8 %copy-done = f32[16,1024]{1,0:T(8,128)S(1)} copy-done((f32[16,1024]{1,0:T(8,128)S(1)}, f32[16,1024]{1,0:T(8,128)}, u32[]{:S(2)}) %copy-start) | copy-done | bytes 65560
  0.8 63.5 %shard_map.28 = f32[16,56,1024]{2,1,0:T(8,128)S(1)} custom-call(f32[56,16,1024]{2,1,0:T(8,128)} %x_ref.1, f32[16,1024]{1,0:T(8,128)S(1)} %copy-done), custom_call_target="tpu_custom_call" | custom-call | tf_op jit(solution)/shard_map/pallas_call | solution.py:440
  64.4 4.0 %copy.3 = f32[56,16,1024]{2,1,0:T(8,128)} copy(f32[56,16,1024]{2,0,1:T(8,128)S(1)} %bitcast.1) | data formatting | bytes 7340032 | tf_op jit(solution)/shard_map/transpose | solution.py:477
Async XLA Ops:
  0.0 0.8 %copy-start = (f32[16,1024]{1,0:T(8,128)S(1)}, f32[16,1024]{1,0:T(8,128)}, u32[]{:S(2)}) copy-start(f32[16,1024]{1,0:T(8,128)} %w_ref.1) | copy-start | bytes 196612
where the time goes:
time: 68.5 us; the launch traced here: 68.4 us
  Pallas kernels  63.5 us (93%)
  local copies, waits for them, and re-layouts  4.8 us (7%)
    pallas_call x1, Pallas kernels, local(): pl.pallas_call(functools.partial(kernel, n_row, n_col, n_band), out_shape...  63.5 us
    transpose x1, local copies, waits for them, and re-layouts, local(): return jnp.transpose(out[:, :bands], (1, 0, 2))  3.96 us

commit v1 on v0

v1 whole, which is shorter than its diff:
```python
import functools

import jax
import jax.numpy as jnp
from jax import lax
from jax.experimental import pallas as pl
from jax.experimental.pallas import tpu as pltpu
from jax.sharding import PartitionSpec as P

ITERS = 4
dual_step = 0.35
primal_step = 0.35
KEEP = 1.0 / (1.0 + primal_step)
GAIN = primal_step / (1.0 + primal_step)
STEP = GAIN * dual_step
LANES = 128
USEFUL = LANES - 2 * ITERS
MESH = pl.DeviceIdType.MESH


def kernel(n_row, n_col, n_band, x_ref, w_ref, out_ref,
           X, WV, N, U, W, QX, QY, HU, HD, E, ER, EL, WT, SC, CY, S, SE, R, RE, RB,
           in_sem, w_sem, ys, yr, xs, xr, zs, zr):
    bands, rows, cols = x_ref.shape
    tiles = N.shape[0]
    groups = bands // 8
    last = rows - 1
    ri = lax.axis_index("row")
    ci = lax.axis_index("col")
    bi = lax.axis_index("band")
    has_up = ri > 0
    has_down = ri < n_row - 1
    has_left = ci > 0
    has_right = ci < n_col - 1
    full = pl.ds(0, bands)

    fetches = [pltpu.make_async_copy(x_ref.at[:, r, :], X.at[r, 0:bands, LANES:LANES + cols], in_sem.at[r])
               for r in range(rows)]
    for copy in fetches:
        copy.start()
    fetch_w = pltpu.make_async_copy(w_ref, WV, w_sem.at[0])
    fetch_w.start()

    barrier = pltpu.get_barrier_semaphore()
    for cond, axis, target in ((has_up, "row", ri - 1), (has_down, "row", ri + 1),
                               (has_left, "col", ci - 1), (has_right, "col", ci + 1)):
        @pl.when(cond)
        def _():
            pl.semaphore_signal(barrier, inc=1, device_id={axis: target}, device_id_type=MESH)
    for d in range(1, n_band):
        pl.semaphore_signal(barrier, inc=1, device_id={"band": lax.rem(bi + d, n_band)}, device_id_type=MESH)
    count = (n_band - 1 + has_up.astype(jnp.int32) + has_down.astype(jnp.int32)
             + has_left.astype(jnp.int32) + has_right.astype(jnp.int32))

    def y_pair(k, j):
        span = pl.ds(0, N.shape[2]) if k == 0 else full
        src = N if k == 0 else W
        up = pltpu.make_async_remote_copy(
            src_ref=src.at[j, 0], dst_ref=HU.at[k, j, span], send_sem=ys.at[0, k, j], recv_sem=yr.at[0, k, j],
            device_id={"row": ri - 1}, device_id_type=MESH)
        down = pltpu.make_async_remote_copy(
            src_ref=src.at[j, last], dst_ref=HD.at[k, j, span], send_sem=ys.at[1, k, j], recv_sem=yr.at[1, k, j],
            device_id={"row": ri + 1}, device_id_type=MESH)
        return up, down

    def y_start(k, j):
        up, down = y_pair(k, j)

        @pl.when(has_up)
        def _():
            up.start()

        @pl.when(has_down)
        def _():
            down.start()

    def y_recv(k, j):
        up, down = y_pair(k, j)

        @pl.when(has_down)
        def _():
            up.wait_recv()

        @pl.when(has_up)
        def _():
            down.wait_recv()

    def y_sent(k, j):
        up, down = y_pair(k, j)

        @pl.when(has_up)
        def _():
            up.wait_send()

        @pl.when(has_down)
        def _():
            down.wait_send()

    def z_copy(k, j, d, part):
        src, dst = ((S, R), (SE, RE))[part]
        return pltpu.make_async_remote_copy(
            src_ref=src.at[k, j], dst_ref=dst.at[k, j, d - 1],
            send_sem=zs.at[k, j, d - 1, part], recv_sem=zr.at[k, j, d - 1, part],
            device_id={"band": lax.rem(bi + d, n_band)}, device_id_type=MESH)

    def z_start(k, j, part):
        for d in range(1, n_band):
            z_copy(k, j, d, part).start()

    def scale_of(weight, squares):
        return jnp.minimum(1.0, weight * lax.rsqrt(1.0 + squares * (1.0 / (GAIN * GAIN))))

    def sync(k, j):
        for part in range(2):
            for d in range(1, n_band):
                z_copy(k, j, d, part).wait_recv()
        acc = S[k, j]
        edge = SE[k, j]
        for d in range(1, n_band):
            acc = acc + R[k, j, d - 1]
            edge = edge + RE[k, j, d - 1]
        SC[j, 0:rows] = scale_of(WT[j, 0:rows], acc)
        SC[j, last:last + 2] = scale_of(WT[j, last:last + 2], edge)

    def to_right(v):
        return pltpu.roll(v, 1, 1)

    def to_left(v):
        return pltpu.roll(v, LANES - 1, 1)

    def squares(qx, qy):
        return jnp.sum(qx * qx + qy * qy, axis=0, keepdims=True)

    def order(i):
        return lax.rem(i + 1, tiles)

    lane = lax.broadcasted_iota(jnp.int32, (8, LANES), 1)
    for j in range(tiles):
        column = ci * cols + j * USEFUL - ITERS + lane
        CY[j] = jnp.where((column >= 0) & (column < n_col * cols - 1), STEP, 0.0)
    S[:, :, last:rows, :] = jnp.zeros((ITERS, tiles, 1, LANES), jnp.float32)
    RB[...] = jnp.zeros_like(RB)

    @pl.when(jnp.logical_not(has_down))
    def _():
        HU[...] = jnp.zeros_like(HU)

    @pl.when(jnp.logical_not(has_up))
    def _():
        HD[...] = jnp.zeros_like(HD)

    @pl.when(jnp.logical_not(has_right))
    def _():
        ER[...] = jnp.zeros_like(ER)

    @pl.when(jnp.logical_not(has_left))
    def _():
        EL[...] = jnp.zeros_like(EL)

    fetch_w.wait()

    def put_weight(r, _):
        X[r, pl.ds(bands, 8), LANES:LANES + cols] = jnp.broadcast_to(WV[pl.ds(r, 1), :], (8, cols))
        return 0
    lax.fori_loop(0, rows, put_weight, 0)

    for copy in fetches:
        copy.wait()

    pitch = 2 * ITERS
    spot = lax.broadcasted_iota(jnp.int32, (8, LANES), 1)

    def pack(g, _):
        span = pl.ds(pl.multiple_of(g * 8, 8), 8)
        acc = jnp.zeros((8, LANES), jnp.float32)
        for r in range(rows):
            at = r * pitch
            head = pltpu.roll(X[r, span, LANES:2 * LANES], at % LANES, 1)
            tail = pltpu.roll(X[r, span, cols:cols + LANES], (at + pitch) % LANES, 1)
            acc = jnp.where((spot >= at) & (spot < at + ITERS), head, acc)
            acc = jnp.where((spot >= at + ITERS) & (spot < at + pitch), tail, acc)
        E[span] = acc
        return 0
    lax.fori_loop(0, groups + 1, pack, 0)

    pl.semaphore_wait(barrier, count)

    e_left = pltpu.make_async_remote_copy(
        src_ref=E, dst_ref=ER, send_sem=xs.at[0], recv_sem=xr.at[0],
        device_id={"col": ci - 1}, device_id_type=MESH)
    e_right = pltpu.make_async_remote_copy(
        src_ref=E, dst_ref=EL, send_sem=xs.at[1], recv_sem=xr.at[1],
        device_id={"col": ci + 1}, device_id_type=MESH)

    @pl.when(has_left)
    def _():
        e_left.start()

    @pl.when(has_right)
    def _():
        e_right.start()

    def begin(j):
        base = j * USEFUL + LANES - ITERS
        at = base // LANES
        turn = base - at * LANES
        lo = pl.ds(pl.multiple_of(at * LANES, LANES), LANES)
        hi = pl.ds(pl.multiple_of(at * LANES + LANES, LANES), LANES)
        near = lax.broadcasted_iota(jnp.int32, (1, LANES), 1) < LANES - turn
        back = lax.rem(LANES - turn, LANES)

        def take(r):
            v = jnp.where(near, pltpu.roll(X[r, :, lo], back, 1), pltpu.roll(X[r, :, hi], back, 1))
            N[j, r] = v
            WT[j, r:r + 1] = v[bands:bands + 1]
            return v[0:bands]

        cy = CY[j, 0:1]
        old = take(0)
        end = take(last)
        y_start(0, j)
        for r in range(1, rows):
            new = take(r) if r < last else end
            qx = STEP * (new - old)
            qy = cy * (to_left(old) - old)
            QX[j, r - 1] = qx
            QY[j, r - 1] = qy
            S[0, j, r - 1:r] = squares(qx, qy)
            old = new
        z_start(0, j, 0)

    def begin_loop(lo, hi):
        def one(i, _):
            begin(order(i))
            return 0
        lax.fori_loop(lo, hi, one, 0)

    inner = sum(1 for j in range(1, tiles) if j * USEFUL + LANES - ITERS <= cols)
    begin_loop(0, inner)

    @pl.when(has_right)
    def _():
        e_left.wait_recv()

    @pl.when(has_left)
    def _():
        e_right.wait_recv()

    def unpack(g, _):
        span = pl.ds(pl.multiple_of(g * 8, 8), 8)
        from_right, from_left = ER[span], EL[span]
        for r in range(rows):
            at = r * pitch
            X[r, span, cols + LANES:cols + 2 * LANES] = pltpu.roll(from_right, (LANES - at) % LANES, 1)
            X[r, span, 0:LANES] = pltpu.roll(from_left, (2 * LANES - at - pitch) % LANES, 1)
        return 0
    lax.fori_loop(0, groups + 1, unpack, 0)
    begin_loop(inner, tiles)

    cx_last = jnp.where(has_down, STEP, 0.0)
    cx_above = jnp.where(has_up, STEP, 0.0)

    def edges(k, j):
        y_recv(k, j)
        field = N if k == 0 else W
        if k == 0:
            WT[j, rows:rows + 1] = HD[0, j, bands:bands + 1]
        cy = CY[j, 0:1]
        end, top = field[j, last, full], field[j, 0, full]
        below, above = HU[k, j, full], HD[k, j, full]
        for i, r, own, nxt, cx in ((0, last, end, below, cx_last), (1, rows, above, top, cx_above)):
            qx = cx * (nxt - own)
            qy = cy * (to_left(own) - own)
            if k > 0:
                sc = SC[j, r:r + 1]
                qx = sc * QX[j, r] + qx
                qy = sc * QY[j, r] + qy
            QX[j, r] = qx
            QY[j, r] = qy
            SE[k, j, i:i + 1] = squares(qx, qy)
        z_start(k, j, 1)

    def edge_loop(k):
        def one(i, _):
            edges(k, order(i))
            return 0
        lax.fori_loop(0, tiles, one, 0)

    edge_loop(0)

    def primal(j, r, px, pu, py, first):
        div = (px - pu) + (py - to_right(py))
        given = N[j, r, full]
        if first:
            return given + div, given
        u = U[j, r]
        return KEEP * u + (GAIN * given + div), u

    def step(k, j):
        first = k == 1
        if k > 1:
            y_sent(k - 1, j)
        sync(k - 1, j)

        def primal_row(r, px, pu, py):
            new, u = primal(j, r, px, pu, py, first)
            U[j, r] = new
            w = 2.0 * new - u
            W[j, r] = w
            return w

        def px_of(r):
            return SC[j, r:r + 1] * QX[j, r]

        def py_of(r):
            return SC[j, r:r + 1] * QY[j, r]

        px, py = px_of(0), py_of(0)
        w = primal_row(0, px, px_of(rows), py)
        end = primal_row(last, px_of(last), px_of(last - 1), py_of(last))
        y_start(k, j)
        cy = CY[j, 0:1]
        for r in range(1, rows):
            if r < last:
                px_new, py_new = px_of(r), py_of(r)
                w_new = primal_row(r, px_new, px, py_new)
            else:
                px_new, py_new, w_new = None, None, end
            qx = px + STEP * (w_new - w)
            qy = py + cy * (to_left(w) - w)
            QX[j, r - 1] = qx
            QY[j, r - 1] = qy
            S[k, j, r - 1:r] = squares(qx, qy)
            px, py, w = px_new, py_new, w_new
        z_start(k, j, 0)

    for k in range(1, ITERS):
        def one(i, _, k=k):
            step(k, order(i))
            return 0
        lax.fori_loop(0, tiles, one, 0)
        edge_loop(k)

    wide_lane = lax.broadcasted_iota(jnp.int32, (1, LANES), 1)

    def finish(j, wrap):
        sync(ITERS - 1, j)
        base = j * USEFUL + LANES - ITERS
        at = base // LANES - 1
        turn = base - (at + 1) * LANES
        if wrap:
            spot, keep = pl.ds(0, LANES), wide_lane >= USEFUL
        else:
            spot, keep = pl.ds(pl.multiple_of(at * LANES, LANES), LANES), wide_lane >= j * USEFUL - at * LANES
        pu = SC[j, rows:rows + 1] * QX[j, rows]
        for r in range(rows):
            sc = SC[j, r:r + 1]
            px = sc * QX[j, r]
            new, _ = primal(j, r, px, pu, sc * QY[j, r], False)
            turned = pltpu.roll(new, turn, 1)
            if wrap:
                out_ref[r, :, spot] = jnp.where(keep, out_ref[r, :, spot], turned)
            else:
                out_ref[r, :, spot] = jnp.where(keep, turned, RB[r])
                RB[r] = turned
            pu = px

    def finish_one(j, _):
        finish(j, False)
        return 0
    lax.fori_loop(1, tiles, finish_one, 0)
    finish(0, True)

    @pl.when(has_left)
    def _():
        e_left.wait_send()

    @pl.when(has_right)
    def _():
        e_right.wait_send()

    def drain(j, _):
        y_sent(0, j)
        y_sent(ITERS - 1, j)
        for k in range(ITERS):
            for d in range(1, n_band):
                for part in range(2):
                    z_copy(k, j, d, part).wait_send()
        return 0
    lax.fori_loop(0, tiles, drain, 0)


def local(n_row, n_col, n_band, noisy, weight_map):
    bands, rows, cols = noisy.shape
    padded = -(-bands // 8) * 8
    x = noisy
    if padded != bands:
        x = jnp.pad(x, ((0, padded - bands), (0, 0), (0, 0)))
    f32 = jnp.float32
    tiles = -(-cols // USEFUL)
    wide = cols + 2 * LANES
    extra = -(-(rows + 1) // 8) * 8
    peers = n_band - 1
    dma = pltpu.SemaphoreType.DMA
    vmem = pltpu.VMEM
    out = pl.pallas_call(
        functools.partial(kernel, n_row, n_col, n_band),
        out_shape=jax.ShapeDtypeStruct((rows, padded, cols), f32),
        in_specs=[pl.BlockSpec(memory_space=pltpu.HBM), pl.BlockSpec(memory_space=pltpu.HBM)],
        out_specs=pl.BlockSpec(memory_space=vmem),
        scratch_shapes=[
            vmem((rows, padded + 8, wide), f32),
            vmem((rows, cols), f32),
            vmem((tiles, rows, padded + 8, LANES), f32),
            vmem((tiles, rows, padded, LANES), f32),
            vmem((tiles, rows, padded, LANES), f32),
            vmem((tiles, rows + 1, padded, LANES), f32),
            vmem((tiles, rows + 1, padded, LANES), f32),
            vmem((ITERS, tiles, padded + 8, LANES), f32),
            vmem((ITERS, tiles, padded + 8, LANES), f32),
            vmem((padded + 8, LANES), f32),
            vmem((padded + 8, LANES), f32),
            vmem((padded + 8, LANES), f32),
            vmem((tiles, extra, LANES), f32),
            vmem((tiles, extra, LANES), f32),
            vmem((tiles, 8, LANES), f32),
            vmem((ITERS, tiles, rows, LANES), f32),
            vmem((ITERS, tiles, 2, LANES), f32),
            vmem((ITERS, tiles, peers, rows, LANES), f32),
            vmem((ITERS, tiles, peers, 2, LANES), f32),
            vmem((rows, padded, LANES), f32),
            dma((rows,)), dma((1,)),
            dma((2, ITERS, tiles)), dma((2, ITERS, tiles)),
            dma((2,)), dma((2,)),
            dma((ITERS, tiles, peers, 2)), dma((ITERS, tiles, peers, 2)),
        ],
        compiler_params=pltpu.CompilerParams(
            collective_id=0, has_side_effects=True, vmem_limit_bytes=50 * 1024 * 1024),
    )(x, weight_map)
    return jnp.transpose(out[:, :bands], (1, 0, 2))


def solution(mesh):
    placed = (P("band", "row", "col"), P("row", "col"))
    sizes = dict(mesh.shape)
    body = functools.partial(local, sizes["row"], sizes["col"], sizes["band"])
    return jax.shard_map(
        body, mesh=mesh, in_specs=placed, out_specs=P("band", "row", "col"), check_vma=False
    )
```

time: 68.5 us -> 60.6 us (0.88)
  Pallas kernels: 63.5 us -> 55.6 us
    pallas_call x1, Pallas kernels: 63.5 us -> 55.6 us  [local(): pl.pallas_call(functools.partial(kernel, n_row, n_col, n_band), out_shape...]
where the time goes in v1:
time: 60.6 us; the launch traced here: 60.4 us
  Pallas kernels  55.6 us (92%)
  local copies, waits for them, and re-layouts  4.8 us (8%)
    pallas_call x1, Pallas kernels, local(): pl.pallas_call(functools.partial(kernel, n_row, n_col, n_band), out_shape...  55.6 us
    transpose x1, local copies, waits for them, and re-layouts, local(): return jnp.transpose(out[:, :bands], (1, 0, 2))  3.96 us

profile of v1, /device:TPU:0, one launch (start us, length us, event | category | flops | bytes accessed | tf_op | source)
XLA Modules:
  0.0 60.4 jit_solution(10095596295108879826)
XLA Ops:
  0.0 0.0 copy-start
  0.0 0.8 %copy-done = f32[16,1024]{1,0:T(8,128)S(1)} copy-done((f32[16,1024]{1,0:T(8,128)S(1)}, f32[16,1024]{1,0:T(8,128)}, u32[]{:S(2)}) %copy-start) | copy-done | bytes 65560
  0.8 55.6 %shard_map.28 = f32[16,56,1024]{2,1,0:T(8,128)S(1)} custom-call(f32[56,16,1024]{2,1,0:T(8,128)} %x_ref.1, f32[16,1024]{1,0:T(8,128)S(1)} %copy-done), custom_call_target="tpu_custom_call" | custom-call | tf_op jit(solution)/shard_map/pallas_call | solution.py:406
  56.5 4.0 %copy.3 = f32[56,16,1024]{2,1,0:T(8,128)} copy(f32[56,16,1024]{2,0,1:T(8,128)S(1)} %bitcast.1) | data formatting | bytes 7340032 | tf_op jit(solution)/shard_map/transpose | solution.py:440
Async XLA Ops:
  0.0 0.8 %copy-start = (f32[16,1024]{1,0:T(8,128)S(1)}, f32[16,1024]{1,0:T(8,128)}, u32[]{:S(2)}) copy-start(f32[16,1024]{1,0:T(8,128)} %w_ref.1) | copy-start | bytes 196612

commit v2 on v1

--- a/solution.py
+++ b/solution.py
@@ -34,7 +34,7 @@
     has_right = ci < n_col - 1
     full = pl.ds(0, bands)
 
-    fetches = [pltpu.make_async_copy(x_ref.at[:, r, :], X.at[r, 0:bands, LANES:LANES + cols], in_sem.at[r])
+    fetches = [pltpu.make_async_copy(x_ref.at[:, r, :], X.at[r, 0:bands, LANES:LANES + cols], in_sem.at[0])
                for r in range(rows)]
     for copy in fetches:
         copy.start()
@@ -56,10 +56,10 @@
         span = pl.ds(0, N.shape[2]) if k == 0 else full
         src = N if k == 0 else W
         up = pltpu.make_async_remote_copy(
-            src_ref=src.at[j, 0], dst_ref=HU.at[k, j, span], send_sem=ys.at[0, k, j], recv_sem=yr.at[0, k, j],
+            src_ref=src.at[j, 0], dst_ref=HU.at[k, j, span], send_sem=ys.at[0, j], recv_sem=yr.at[0, k % 2, j],
             device_id={"row": ri - 1}, device_id_type=MESH)
         down = pltpu.make_async_remote_copy(
-            src_ref=src.at[j, last], dst_ref=HD.at[k, j, span], send_sem=ys.at[1, k, j], recv_sem=yr.at[1, k, j],
+            src_ref=src.at[j, last], dst_ref=HD.at[k, j, span], send_sem=ys.at[1, j], recv_sem=yr.at[1, k % 2, j],
             device_id={"row": ri + 1}, device_id_type=MESH)
         return up, down
 
@@ -96,24 +96,28 @@
         def _():
             down.wait_send()
 
-    def z_copy(k, j, d, part):
+    def z_start(k, j, part):
         src, dst = ((S, R), (SE, RE))[part]
-        return pltpu.make_async_remote_copy(
-            src_ref=src.at[k, j], dst_ref=dst.at[k, j, d - 1],
-            send_sem=zs.at[k, j, d - 1, part], recv_sem=zr.at[k, j, d - 1, part],
-            device_id={"band": lax.rem(bi + d, n_band)}, device_id_type=MESH)
-
-    def z_start(k, j, part):
         for d in range(1, n_band):
-            z_copy(k, j, d, part).start()
+            pltpu.make_async_remote_copy(
+                src_ref=src.at[k, j], dst_ref=dst.at[k, j, d - 1],
+                send_sem=zs.at[part], recv_sem=zr.at[k % 2, j, part],
+                device_id={"band": lax.rem(bi + d, n_band)}, device_id_type=MESH).start()
+
+    def z_recv(k, j, part):
+        dst = (R, RE)[part].at[k, j]
+        pltpu.make_async_copy(dst, dst, zr.at[k % 2, j, part]).wait()
+
+    def z_sent(part):
+        dst = (R, RE)[part]
+        pltpu.make_async_copy(dst, dst, zs.at[part]).wait()
 
     def scale_of(weight, squares):
         return jnp.minimum(1.0, weight * lax.rsqrt(1.0 + squares * (1.0 / (GAIN * GAIN))))
 
     def sync(k, j):
-        for part in range(2):
-            for d in range(1, n_band):
-                z_copy(k, j, d, part).wait_recv()
+        z_recv(k, j, 0)
+        z_recv(k, j, 1)
         acc = S[k, j]
         edge = SE[k, j]
         for d in range(1, n_band):
@@ -164,8 +168,8 @@
         return 0
     lax.fori_loop(0, rows, put_weight, 0)
 
-    for copy in fetches:
-        copy.wait()
+    whole = X.at[:, 0:bands, LANES:LANES + cols]
+    pltpu.make_async_copy(whole, whole, in_sem.at[0]).wait()
 
     pitch = 2 * ITERS
     spot = lax.broadcasted_iota(jnp.int32, (8, LANES), 1)
@@ -229,33 +233,19 @@
             old = new
         z_start(0, j, 0)
 
-    def begin_loop(lo, hi):
-        def one(i, _):
-            begin(order(i))
-            return 0
-        lax.fori_loop(lo, hi, one, 0)
-
-    inner = sum(1 for j in range(1, tiles) if j * USEFUL + LANES - ITERS <= cols)
-    begin_loop(0, inner)
-
-    @pl.when(has_right)
-    def _():
-        e_left.wait_recv()
-
-    @pl.when(has_left)
-    def _():
-        e_right.wait_recv()
-
-    def unpack(g, _):
-        span = pl.ds(pl.multiple_of(g * 8, 8), 8)
-        from_right, from_left = ER[span], EL[span]
-        for r in range(rows):
-            at = r * pitch
-            X[r, span, cols + LANES:cols + 2 * LANES] = pltpu.roll(from_right, (LANES - at) % LANES, 1)
-            X[r, span, 0:LANES] = pltpu.roll(from_left, (2 * LANES - at - pitch) % LANES, 1)
-        return 0
-    lax.fori_loop(0, groups + 1, unpack, 0)
-    begin_loop(inner, tiles)
+    lag = min(3, tiles)
+
+    def sweep(lo, hi, act, k):
+        def span(lo, hi, k_edge):
+            def one(i, _):
+                act(order(i))
+                if k_edge >= 0:
+                    edges(k_edge, order(i + tiles - lag if k_edge < k else i - lag))
+                return 0
+            if lo < hi:
+                lax.fori_loop(lo, hi, one, 0)
+        span(lo, min(hi, lag), k - 1)
+        span(max(lo, lag), hi, k)
 
     cx_last = jnp.where(has_down, STEP, 0.0)
     cx_above = jnp.where(has_up, STEP, 0.0)
@@ -280,13 +270,27 @@
             SE[k, j, i:i + 1] = squares(qx, qy)
         z_start(k, j, 1)
 
-    def edge_loop(k):
-        def one(i, _):
-            edges(k, order(i))
-            return 0
-        lax.fori_loop(0, tiles, one, 0)
-
-    edge_loop(0)
+    inner = sum(1 for j in range(1, tiles) if j * USEFUL + LANES - ITERS <= cols)
+    sweep(0, inner, begin, 0)
+
+    @pl.when(has_right)
+    def _():
+        e_left.wait_recv()
+
+    @pl.when(has_left)
+    def _():
+        e_right.wait_recv()
+
+    def unpack(g, _):
+        span = pl.ds(pl.multiple_of(g * 8, 8), 8)
+        from_right, from_left = ER[span], EL[span]
+        for r in range(rows):
+            at = r * pitch
+            X[r, span, cols + LANES:cols + 2 * LANES] = pltpu.roll(from_right, (LANES - at) % LANES, 1)
+            X[r, span, 0:LANES] = pltpu.roll(from_left, (2 * LANES - at - pitch) % LANES, 1)
+        return 0
+    lax.fori_loop(0, groups + 1, unpack, 0)
+    sweep(inner, tiles, begin, 0)
 
     def primal(j, r, px, pu, py, first):
         div = (px - pu) + (py - to_right(py))
@@ -298,9 +302,8 @@
 
     def step(k, j):
         first = k == 1
-        if k > 1:
-            y_sent(k - 1, j)
         sync(k - 1, j)
+        y_sent(k - 1, j)
 
         def primal_row(r, px, pu, py):
             new, u = primal(j, r, px, pu, py, first)
@@ -335,11 +338,7 @@
         z_start(k, j, 0)
 
     for k in range(1, ITERS):
-        def one(i, _, k=k):
-            step(k, order(i))
-            return 0
-        lax.fori_loop(0, tiles, one, 0)
-        edge_loop(k)
+        sweep(0, tiles, functools.partial(step, k), k)
 
     wide_lane = lax.broadcasted_iota(jnp.int32, (1, LANES), 1)
 
@@ -353,22 +352,30 @@
         else:
             spot, keep = pl.ds(pl.multiple_of(at * LANES, LANES), LANES), wide_lane >= j * USEFUL - at * LANES
         pu = SC[j, rows:rows + 1] * QX[j, rows]
-        for r in range(rows):
-            sc = SC[j, r:r + 1]
-            px = sc * QX[j, r]
-            new, _ = primal(j, r, px, pu, sc * QY[j, r], False)
-            turned = pltpu.roll(new, turn, 1)
+        for low in range(0, rows, 8):
+            done = []
+            for r in range(low, low + 8):
+                sc = SC[j, r:r + 1]
+                px = sc * QX[j, r]
+                new, _ = primal(j, r, px, pu, sc * QY[j, r], False)
+                turned = pltpu.roll(new, turn, 1)
+                if wrap:
+                    done.append(turned)
+                else:
+                    done.append(jnp.where(keep, turned, RB[r]))
+                    RB[r] = turned
+                pu = px
+            block = jnp.swapaxes(jnp.stack(done, axis=0), 0, 1)
             if wrap:
-                out_ref[r, :, spot] = jnp.where(keep, out_ref[r, :, spot], turned)
-            else:
-                out_ref[r, :, spot] = jnp.where(keep, turned, RB[r])
-                RB[r] = turned
-            pu = px
-
-    def finish_one(j, _):
-        finish(j, False)
+                block = jnp.where(keep[None], out_ref[:, low:low + 8, spot], block)
+            out_ref[:, low:low + 8, spot] = block
+
+    def finish_rest(i, _):
+        finish(i + 1, False)
         return 0
-    lax.fori_loop(1, tiles, finish_one, 0)
+
+    sweep(0, lag, lambda j: finish(j, False), ITERS)
+    lax.fori_loop(lag, tiles - 1, finish_rest, 0)
     finish(0, True)
 
     @pl.when(has_left)
@@ -379,13 +386,11 @@
     def _():
         e_right.wait_send()
 
+    z_sent(0)
+    z_sent(1)
+
     def drain(j, _):
-        y_sent(0, j)
         y_sent(ITERS - 1, j)
-        for k in range(ITERS):
-            for d in range(1, n_band):
-                for part in range(2):
-                    z_copy(k, j, d, part).wait_send()
         return 0
     lax.fori_loop(0, tiles, drain, 0)
 
@@ -405,7 +410,7 @@
     vmem = pltpu.VMEM
     out = pl.pallas_call(
         functools.partial(kernel, n_row, n_col, n_band),
-        out_shape=jax.ShapeDtypeStruct((rows, padded, cols), f32),
+        out_shape=jax.ShapeDtypeStruct((padded, rows, cols), f32),
         in_specs=[pl.BlockSpec(memory_space=pltpu.HBM), pl.BlockSpec(memory_space=pltpu.HBM)],
         out_specs=pl.BlockSpec(memory_space=vmem),
         scratch_shapes=[
@@ -429,15 +434,15 @@
             vmem((ITERS, tiles, peers, rows, LANES), f32),
             vmem((ITERS, tiles, peers, 2, LANES), f32),
             vmem((rows, padded, LANES), f32),
-            dma((rows,)), dma((1,)),
-            dma((2, ITERS, tiles)), dma((2, ITERS, tiles)),
+            dma((1,)), dma((1,)),
+            dma((2, tiles)), dma((2, 2, tiles)),
             dma((2,)), dma((2,)),
-            dma((ITERS, tiles, peers, 2)), dma((ITERS, tiles, peers, 2)),
+            dma((2,)), dma((2, tiles, 2)),
         ],
         compiler_params=pltpu.CompilerParams(
             collective_id=0, has_side_effects=True, vmem_limit_bytes=50 * 1024 * 1024),
     )(x, weight_map)
-    return jnp.transpose(out[:, :bands], (1, 0, 2))
+    return out[:bands]
 
 
 def solution(mesh):

time: 60.6 us -> 47.5 us (0.78)
  Pallas kernels: 55.6 us -> 44.6 us
  local copies, waits for them, and re-layouts: 4.8 us -> 2.68 us
    pallas_call x1, Pallas kernels: 55.6 us -> 44.6 us  [local(): pl.pallas_call(functools.partial(kernel, n_row, n_col, n_band), out_shape...]
    transpose x1 -> x0, local copies, waits for them, and re-layouts: 3.96 us -> none  [local(): return jnp.transpose(out[:, :bands], (1, 0, 2))]
    unnamed x2 -> x3, local copies, waits for them, and re-layouts: 0.84 us -> 2.68 us
where the time goes in v2:
time: 47.5 us; the launch traced here: 47.3 us
  Pallas kernels  44.6 us (94%)
  local copies, waits for them, and re-layouts  2.68 us (6%)
    pallas_call x1, Pallas kernels, local(): pl.pallas_call(functools.partial(kernel, n_row, n_col, n_band), out_shape...  44.6 us
    unnamed x3, local copies, waits for them, and re-layouts  2.68 us

profile of v2, /device:TPU:0, one launch (start us, length us, event | category | flops | bytes accessed | tf_op | source)
XLA Modules:
  0.0 47.3 jit_solution(12045585074238699694)
XLA Ops:
  0.0 0.0 copy-start
  0.0 0.8 %copy-done = f32[16,1024]{1,0:T(8,128)S(1)} copy-done((f32[16,1024]{1,0:T(8,128)S(1)}, f32[16,1024]{1,0:T(8,128)}, u32[]{:S(2)}) %copy-start) | copy-done | bytes 65560
  0.8 44.6 %shard_map.28 = f32[56,16,1024]{2,1,0:T(8,128)S(1)} custom-call(f32[56,16,1024]{2,1,0:T(8,128)} %x_ref.1, f32[16,1024]{1,0:T(8,128)S(1)} %copy-done), custom_call_target="tpu_custom_call" | custom-call | tf_op jit(solution)/shard_map/pallas_call | solution.py:411
  45.5 1.8 %copy.4 = f32[56,16,1024]{2,1,0:T(8,128)} copy(f32[56,16,1024]{2,1,0:T(8,128)S(1)} %shard_map.28) | data formatting | bytes 7340032
Async XLA Ops:
  0.0 0.8 %copy-start = (f32[16,1024]{1,0:T(8,128)S(1)}, f32[16,1024]{1,0:T(8,128)}, u32[]{:S(2)}) copy-start(f32[16,1024]{1,0:T(8,128)} %w_ref.1) | copy-start | bytes 196612

commit v3 on v2

--- a/solution.py
+++ b/solution.py
@@ -34,12 +34,19 @@
     has_right = ci < n_col - 1
     full = pl.ds(0, bands)
 
-    fetches = [pltpu.make_async_copy(x_ref.at[:, r, :], X.at[r, 0:bands, LANES:LANES + cols], in_sem.at[0])
-               for r in range(rows)]
-    for copy in fetches:
-        copy.start()
+    middle = max(1, cols // LANES // 2) * LANES
+    parts = [(lo, hi) for lo, hi in ((0, middle), (middle, cols)) if lo < hi]
+
     fetch_w = pltpu.make_async_copy(w_ref, WV, w_sem.at[0])
     fetch_w.start()
+    for p, (lo, hi) in enumerate(parts):
+        for r in range(rows):
+            pltpu.make_async_copy(x_ref.at[:, r, lo:hi], X.at[r, 0:bands, LANES + lo:LANES + hi], in_sem.at[p]).start()
+
+    def fetched(p):
+        lo, hi = parts[p]
+        whole = X.at[:, 0:bands, LANES + lo:LANES + hi]
+        pltpu.make_async_copy(whole, whole, in_sem.at[p]).wait()
 
     barrier = pltpu.get_barrier_semaphore()
     for cond, axis, target in ((has_up, "row", ri - 1), (has_down, "row", ri + 1),
@@ -168,8 +175,7 @@
         return 0
     lax.fori_loop(0, rows, put_weight, 0)
 
-    whole = X.at[:, 0:bands, LANES:LANES + cols]
-    pltpu.make_async_copy(whole, whole, in_sem.at[0]).wait()
+    fetched(0)
 
     pitch = 2 * ITERS
     spot = lax.broadcasted_iota(jnp.int32, (8, LANES), 1)
@@ -185,7 +191,6 @@
             acc = jnp.where((spot >= at + ITERS) & (spot < at + pitch), tail, acc)
         E[span] = acc
         return 0
-    lax.fori_loop(0, groups + 1, pack, 0)
 
     pl.semaphore_wait(barrier, count)
 
@@ -196,15 +201,7 @@
         src_ref=E, dst_ref=EL, send_sem=xs.at[1], recv_sem=xr.at[1],
         device_id={"col": ci + 1}, device_id_type=MESH)
 
-    @pl.when(has_left)
-    def _():
-        e_left.start()
-
-    @pl.when(has_right)
-    def _():
-        e_right.start()
-
-    def begin(j):
+    def begin(j, between):
         base = j * USEFUL + LANES - ITERS
         at = base // LANES
         turn = base - at * LANES
@@ -223,6 +220,7 @@
         old = take(0)
         end = take(last)
         y_start(0, j)
+        between()
         for r in range(1, rows):
             new = take(r) if r < last else end
             qx = STEP * (new - old)
@@ -233,14 +231,15 @@
             old = new
         z_start(0, j, 0)
 
-    lag = min(3, tiles)
+    lag = min(4, tiles - 1)
 
     def sweep(lo, hi, act, k):
         def span(lo, hi, k_edge):
             def one(i, _):
-                act(order(i))
-                if k_edge >= 0:
-                    edges(k_edge, order(i + tiles - lag if k_edge < k else i - lag))
+                def middle_of():
+                    if k_edge >= 0:
+                        edges(k_edge, order(i + tiles - lag if k_edge < k else i - lag))
+                act(order(i), middle_of)
                 return 0
             if lo < hi:
                 lax.fori_loop(lo, hi, one, 0)
@@ -271,7 +270,21 @@
         z_start(k, j, 1)
 
     inner = sum(1 for j in range(1, tiles) if j * USEFUL + LANES - ITERS <= cols)
-    sweep(0, inner, begin, 0)
+    early = sum(1 for j in (1, 2) if j < tiles and (j * USEFUL + LANES - ITERS) // LANES + 1 <= middle // LANES)
+    sweep(0, early, begin, 0)
+    for p in range(1, len(parts)):
+        fetched(p)
+    lax.fori_loop(0, groups + 1, pack, 0)
+
+    @pl.when(has_left)
+    def _():
+        e_left.start()
+
+    @pl.when(has_right)
+    def _():
+        e_right.start()
+
+    sweep(early, inner, begin, 0)
 
     @pl.when(has_right)
     def _():
@@ -300,7 +313,7 @@
         u = U[j, r]
         return KEEP * u + (GAIN * given + div), u
 
-    def step(k, j):
+    def step(k, j, between):
         first = k == 1
         sync(k - 1, j)
         y_sent(k - 1, j)
@@ -322,6 +335,7 @@
         w = primal_row(0, px, px_of(rows), py)
         end = primal_row(last, px_of(last), px_of(last - 1), py_of(last))
         y_start(k, j)
+        between()
         cy = CY[j, 0:1]
         for r in range(1, rows):
             if r < last:
@@ -342,7 +356,8 @@
 
     wide_lane = lax.broadcasted_iota(jnp.int32, (1, LANES), 1)
 
-    def finish(j, wrap):
+    def finish(j, between, wrap=False):
+        between()
         sync(ITERS - 1, j)
         base = j * USEFUL + LANES - ITERS
         at = base // LANES - 1
@@ -357,8 +372,9 @@
             for r in range(low, low + 8):
                 sc = SC[j, r:r + 1]
                 px = sc * QX[j, r]
-                new, _ = primal(j, r, px, pu, sc * QY[j, r], False)
-                turned = pltpu.roll(new, turn, 1)
+                py = sc * QY[j, r]
+                now = KEEP * U[j, r] + (GAIN * N[j, r, full] + ((px - pu) + py))
+                turned = pltpu.roll(now, turn, 1) - pltpu.roll(py, lax.rem(turn + 1, LANES), 1)
                 if wrap:
                     done.append(turned)
                 else:
@@ -371,12 +387,12 @@
             out_ref[:, low:low + 8, spot] = block
 
     def finish_rest(i, _):
-        finish(i + 1, False)
+        finish(i + 1, lambda: None)
         return 0
 
-    sweep(0, lag, lambda j: finish(j, False), ITERS)
+    sweep(0, lag, finish, ITERS)
     lax.fori_loop(lag, tiles - 1, finish_rest, 0)
-    finish(0, True)
+    finish(0, lambda: None, True)
 
     @pl.when(has_left)
     def _():
@@ -434,7 +450,7 @@
             vmem((ITERS, tiles, peers, rows, LANES), f32),
             vmem((ITERS, tiles, peers, 2, LANES), f32),
             vmem((rows, padded, LANES), f32),
-            dma((1,)), dma((1,)),
+            dma((2,)), dma((1,)),
             dma((2, tiles)), dma((2, 2, tiles)),
             dma((2,)), dma((2,)),
             dma((2,)), dma((2, tiles, 2)),

time: 47.5 us -> 45.2 us (0.952)
  Pallas kernels: 44.6 us -> 42.3 us
    pallas_call x1, Pallas kernels: 44.6 us -> 42.3 us  [local(): pl.pallas_call(functools.partial(kernel, n_row, n_col, n_band), out_shape...]
where the time goes in v3:
time: 45.2 us; the launch traced here: 45 us
  Pallas kernels  42.3 us (94%)
  local copies, waits for them, and re-layouts  2.68 us (6%)
    pallas_call x1, Pallas kernels, local(): pl.pallas_call(functools.partial(kernel, n_row, n_col, n_band), out_shape...  42.3 us
    unnamed x3, local copies, waits for them, and re-layouts  2.68 us

profile of v3, /device:TPU:0, one launch (start us, length us, event | category | flops | bytes accessed | tf_op | source)
XLA Modules:
  0.0 45.0 jit_solution(6140440818755015887)
XLA Ops:
  0.0 0.0 copy-start
  0.0 0.8 %copy-done = f32[16,1024]{1,0:T(8,128)S(1)} copy-done((f32[16,1024]{1,0:T(8,128)S(1)}, f32[16,1024]{1,0:T(8,128)}, u32[]{:S(2)}) %copy-start) | copy-done | bytes 65560
  0.8 42.3 %shard_map.28 = f32[56,16,1024]{2,1,0:T(8,128)S(1)} custom-call(f32[56,16,1024]{2,1,0:T(8,128)} %x_ref.1, f32[16,1024]{1,0:T(8,128)S(1)} %copy-done), custom_call_target="tpu_custom_call" | custom-call | tf_op jit(solution)/shard_map/pallas_call | solution.py:427
  43.1 1.8 %copy.4 = f32[56,16,1024]{2,1,0:T(8,128)} copy(f32[56,16,1024]{2,1,0:T(8,128)S(1)} %shard_map.28) | data formatting | bytes 7340032
Async XLA Ops:
  0.0 0.8 %copy-start = (f32[16,1024]{1,0:T(8,128)S(1)}, f32[16,1024]{1,0:T(8,128)}, u32[]{:S(2)}) copy-start(f32[16,1024]{1,0:T(8,128)} %w_ref.1) | copy-start | bytes 196612

commit v4 on v3

--- a/solution.py
+++ b/solution.py
@@ -105,18 +105,19 @@
 
     def z_start(k, j, part):
         src, dst = ((S, R), (SE, RE))[part]
+        span = pl.ds(0, (last, 2)[part])
         for d in range(1, n_band):
             pltpu.make_async_remote_copy(
-                src_ref=src.at[k, j], dst_ref=dst.at[k, j, d - 1],
+                src_ref=src.at[k, j, span], dst_ref=dst.at[k, j, d - 1, span],
                 send_sem=zs.at[part], recv_sem=zr.at[k % 2, j, part],
                 device_id={"band": lax.rem(bi + d, n_band)}, device_id_type=MESH).start()
 
     def z_recv(k, j, part):
-        dst = (R, RE)[part].at[k, j]
+        dst = (R, RE)[part].at[k, j, :, pl.ds(0, (last, 2)[part])]
         pltpu.make_async_copy(dst, dst, zr.at[k % 2, j, part]).wait()
 
     def z_sent(part):
-        dst = (R, RE)[part]
+        dst = (R, RE)[part].at[:, :, :, pl.ds(0, (last, 2)[part])]
         pltpu.make_async_copy(dst, dst, zs.at[part]).wait()
 
     def scale_of(weight, squares):
@@ -125,12 +126,12 @@
     def sync(k, j):
         z_recv(k, j, 0)
         z_recv(k, j, 1)
-        acc = S[k, j]
+        acc = S[k, j, 0:last]
         edge = SE[k, j]
         for d in range(1, n_band):
-            acc = acc + R[k, j, d - 1]
+            acc = acc + R[k, j, d - 1, 0:last]
             edge = edge + RE[k, j, d - 1]
-        SC[j, 0:rows] = scale_of(WT[j, 0:rows], acc)
+        SC[j, 0:last] = scale_of(WT[j, 0:last], acc)
         SC[j, last:last + 2] = scale_of(WT[j, last:last + 2], edge)
 
     def to_right(v):
@@ -149,7 +150,6 @@
     for j in range(tiles):
         column = ci * cols + j * USEFUL - ITERS + lane
         CY[j] = jnp.where((column >= 0) & (column < n_col * cols - 1), STEP, 0.0)
-    S[:, :, last:rows, :] = jnp.zeros((ITERS, tiles, 1, LANES), jnp.float32)
     RB[...] = jnp.zeros_like(RB)
 
     @pl.when(jnp.logical_not(has_down))
@@ -331,24 +331,41 @@
         def py_of(r):
             return SC[j, r:r + 1] * QY[j, r]
 
-        px, py = px_of(0), py_of(0)
-        w = primal_row(0, px, px_of(rows), py)
-        end = primal_row(last, px_of(last), px_of(last - 1), py_of(last))
+        primal_row(0, px_of(0), px_of(rows), py_of(0))
+        primal_row(last, px_of(last), px_of(last - 1), py_of(last))
         y_start(k, j)
         between()
         cy = CY[j, 0:1]
+        total = [0.0] * last
+        for g in range(groups):
+            span = pl.ds(g * 8, 8)
+            px = SC[j, 0:1] * QX[j, 0, span]
+            py = SC[j, 0:1] * QY[j, 0, span]
+            w = W[j, 0, span]
+            for r in range(1, rows):
+                if r < last:
+                    sc = SC[j, r:r + 1]
+                    px_new = sc * QX[j, r, span]
+                    py_new = sc * QY[j, r, span]
+                    div = (px_new - px) + (py_new - to_right(py_new))
+                    given = N[j, r, span]
+                    if first:
+                        u, new = given, given + div
+                    else:
+                        u = U[j, r, span]
+                        new = KEEP * u + (GAIN * given + div)
+                    U[j, r, span] = new
+                    w_new = 2.0 * new - u
+                else:
+                    px_new, py_new, w_new = None, None, W[j, last, span]
+                qx = px + STEP * (w_new - w)
+                qy = py + cy * (to_left(w) - w)
+                QX[j, r - 1, span] = qx
+                QY[j, r - 1, span] = qy
+                total[r - 1] = total[r - 1] + (qx * qx + qy * qy)
+                px, py, w = px_new, py_new, w_new
         for r in range(1, rows):
-            if r < last:
-                px_new, py_new = px_of(r), py_of(r)
-                w_new = primal_row(r, px_new, px, py_new)
-            else:
-                px_new, py_new, w_new = None, None, end
-            qx = px + STEP * (w_new - w)
-            qy = py + cy * (to_left(w) - w)
-            QX[j, r - 1] = qx
-            QY[j, r - 1] = qy
-            S[k, j, r - 1:r] = squares(qx, qy)
-            px, py, w = px_new, py_new, w_new
+            S[k, j, r - 1:r] = jnp.sum(total[r - 1], axis=0, keepdims=True)
         z_start(k, j, 0)
 
     for k in range(1, ITERS):

time: 45.2 us -> 44.6 us (0.987)
  Pallas kernels: 42.3 us -> 41.8 us
    pallas_call x1, Pallas kernels: 42.3 us -> 41.8 us  [local(): pl.pallas_call(functools.partial(kernel, n_row, n_col, n_band), out_shape...]
where the time goes in v4:
time: 44.6 us; the launch traced here: 44.5 us
  Pallas kernels  41.8 us (94%)
  local copies, waits for them, and re-layouts  2.68 us (6%)
    pallas_call x1, Pallas kernels, local(): pl.pallas_call(functools.partial(kernel, n_row, n_col, n_band), out_shape...  41.8 us
    unnamed x3, local copies, waits for them, and re-layouts  2.68 us

profile of v4, /device:TPU:0, one launch (start us, length us, event | category | flops | bytes accessed | tf_op | source)
XLA Modules:
  0.0 44.5 jit_solution(901761265150998664)
XLA Ops:
  0.0 0.0 copy-start
  0.0 0.8 %copy-done = f32[16,1024]{1,0:T(8,128)S(1)} copy-done((f32[16,1024]{1,0:T(8,128)S(1)}, f32[16,1024]{1,0:T(8,128)}, u32[]{:S(2)}) %copy-start) | copy-done | bytes 65560
  0.8 41.8 %shard_map.28 = f32[56,16,1024]{2,1,0:T(8,128)S(1)} custom-call(f32[56,16,1024]{2,1,0:T(8,128)} %x_ref.1, f32[16,1024]{1,0:T(8,128)S(1)} %copy-done), custom_call_target="tpu_custom_call" | custom-call | tf_op jit(solution)/shard_map/pallas_call | solution.py:444
  42.6 1.8 %copy.4 = f32[56,16,1024]{2,1,0:T(8,128)} copy(f32[56,16,1024]{2,1,0:T(8,128)S(1)} %shard_map.28) | data formatting | bytes 7340032
Async XLA Ops:
  0.0 0.8 %copy-start = (f32[16,1024]{1,0:T(8,128)S(1)}, f32[16,1024]{1,0:T(8,128)}, u32[]{:S(2)}) copy-start(f32[16,1024]{1,0:T(8,128)} %w_ref.1) | copy-start | bytes 196612
